TPU v7x, 256 devices: a whole 4x4x8 slice. The times are simulated.
256 devices in a mesh: bank: 64 (over z, y, core), zero: 4 (over x).
Axes of the slice: x: 4, y: 4, z: 8, core: 2. Of those that a mesh axis runs over, the one named last changes fastest.
Arguments:
- train_down: float32 [128, 768, 2048], P('bank', None, 'zero'), may hold values from -0.3125 to 0.3125
- other_down: float32 [128, 768, 2048], P('bank', None, 'zero'), may hold values from -0.21875 to 0.21875
- router_weight: float32 [2048, 128], P('zero', 'bank'), may hold values from -0.125 to 0.125
- router_gain: float32 [2048], P('zero'), may hold values from 0.25 to 1.75
Outputs:
- ready_down: bfloat16 [128, 768, 2048], P('bank')
- scale_down: float32 [128, 768], P('bank')
- serve_router: bfloat16 [2048, 128], replicated
- latest_down: float32 [128, 768, 2048], P('bank', None, 'zero')
All inputs are finite; a program needn't handle non-finite values. Where the computation divides by a largest or mean magnitude, that divisor is 1e-20 or more.
Results may differ from a plain program's by a relative error of at most 0.001.
Values may be sent and summed in bfloat16 or wider, within the bound.
No kernel may reach another device: no remote copies, remote signals or barrier semaphores. Data moves between devices by JAX's collectives and lax.ppermute only.
A program may use at most 128 MiB of HBM per device.

v0:
```python
import jax
import jax.numpy as jnp
from jax import lax
from jax.sharding import Mesh
from jax.sharding import PartitionSpec as P

D_MODEL = 2048
BANK = ("bank_0", "bank_1", "bank_2")


def copy_for_each(x, axis):
    devices = lax.axis_size(axis)
    return lax.all_to_all(jnp.broadcast_to(x[None], (devices, *x.shape)), axis, 0, 0, tiled=True)


def of_everyone(x, axis):
    return copy_for_each(x, axis).sum(axis=0)


def in_order(blocks, dim):
    blocks = jnp.moveaxis(blocks, 0, dim)
    shape = blocks.shape
    return blocks.reshape(*shape[:dim], shape[dim] * shape[dim + 1], *shape[dim + 2 :])


def all_blocks(x, axes, turns):
    blocks = x
    for k in turns:
        blocks = lax.all_gather(blocks, axes[k])
    done = turns[::-1]
    back = [done.index(k) for k in range(len(axes))]
    blocks = blocks.transpose(*back, *range(len(axes), blocks.ndim))
    return blocks.reshape(-1, *x.shape)


def gather_axes(x, axes, turns, dim):
    return in_order(all_blocks(x, axes, turns), dim)


def shards(train_down, other_down, router_weight, router_gain):
    latest_down = 0.5 * other_down + 0.5 * train_down
    total_down = of_everyone(jnp.sum(jnp.abs(latest_down), axis=2), "zero")
    scale_down = total_down / D_MODEL
    narrow_down = (latest_down / jnp.expand_dims(scale_down, 2)).astype(jnp.bfloat16)
    ready_down = lax.all_gather(narrow_down, "zero", axis=2, tiled=True)
    part_router = (router_weight * router_gain[:, None]).astype(jnp.bfloat16)
    row_router = lax.all_gather(part_router, "zero", axis=0, tiled=True)
    serve_router = gather_axes(row_router, BANK, (1, 0, 2), 1)
    return (ready_down, scale_down, serve_router, latest_down)


def solution(mesh):
    split = Mesh(
        mesh.devices.reshape(8, 4, 2, mesh.shape["zero"]), ("bank_0", "bank_1", "bank_2", "zero")
    )
    placed = (P(BANK, None, "zero"), P(BANK, None, "zero"), P("zero", BANK), P("zero"))
    return jax.shard_map(
        shards,
        mesh=split,
        in_specs=placed,
        out_specs=(P(BANK, None, None), P(BANK, None), P(), P(BANK, None, "zero")),
        check_vma=False,
    )
```

profile of v0, /device:TPU:1, one launch (start us, length us, event | category | flops | bytes accessed | tf_op | source)
XLA Modules:
  0.0 105.1 jit_solution(9432049307572382526)
XLA Ops:
  7.2 0.0 all-gather.5.cloned.1.call-start
  7.2 3.3 %abs_reduce_fusion = (f32[2,768]{1,0:T(2,128)S(1)}, f32[2,768,512]{2,1,0:T(8,128)S(1)}) fusion(f32[2,768,512]{2,1,0:T(8,128)} %param.5, f32[2,768,512]{2,1,0:T(8,128)} %param.4), kind=kLoop, calls=%fused_computation.1 | loop fusion | flops 3144192 | bytes 9443328 | tf_op jit(solution)/shard_map/reduce_sum | solution.py:42
  10.6 0.0 copy-start
  10.6 8.9 %all_to_all.5 = f32[4,2,768]{2,1,0:T(2,128)S(1)} all-to-all(f32[4,2,768]{2,1,0:T(2,128)S(1)} %broadcast_in_dim.2), channel_id=1, replica_groups=mesh['bank_0'=8,'bank_1'=4,'bank_2'=2,'zero'=4] {'zero'}, dimensions={0} | all-to-all | bytes 49152 | tf_op jit(solution)/shard_map/all_to_all | solution.py:13
  19.5 0.0 copy-start.1
  19.5 0.0 copy-start.2
  19.5 0.0 copy-start.3
  19.5 1.4 %divide_convert_fusion = bf16[2,768,512]{2,1,0:T(8,128)(2,1)} fusion(f32[2,768,512]{2,1,0:T(8,128)S(1)} %get-tuple-element.33, f32[2,768]{1,0:T(2,128)S(1)} %broadcast_multiply_fusion), kind=kLoop, calls=%fused_computation | loop fusion | flops 1572864 | bytes 4724736 | tf_op jit(solution)/shard_map/convert_element_type | solution.py:44
  21.0 0.0 all-gather.5.cloned.1.call-update
  21.0 0.0 copy-done
  21.0 0.0 copy-done.1
  21.0 0.0 copy-done.2
  21.0 0.0 copy-done.3
  21.1 8.1 %all_gather.25 = bf16[2048,2]{0,1:T(2,128)(2,1)S(1)} all-gather(bf16[512,2]{0,1:T(2,128)(2,1)S(1)} %multiply_convert_fusion), channel_id=1, replica_groups=mesh['bank_0'=8,'bank_1'=4,'bank_2'=2,'zero'=4] {'zero'}, dimensions={0}, use_global_device_ids=true | all-gather | bytes 10240 | tf_op jit(solution)/shard_map/all_gather | solution.py:47
  29.2 9.5 %all-gather = bf16[8192,2]{0,1:T(2,128)(2,1)S(1)} all-gather(bf16[2048,2]{0,1:T(2,128)(2,1)S(1)} %all_gather.25), channel_id=2, replica_groups=mesh['bank_0'=8,'bank_1'=4,'bank_2'=2,'zero'=4] {'bank_1'}, dimensions={0}, use_global_device_ids=true | all-gather | bytes 40960 | tf_op jit(solution)/shard_map/all_gather | solution.py:29
  38.7 24.8 %all-gather.1 = bf16[32,2048,2]{1,2,0:T(2,128)(2,1)S(1)} all-gather(bf16[4,2048,2]{1,2,0:T(2,128)(2,1)S(1)} %bitcast.15), channel_id=3, replica_groups=mesh['bank_0'=8,'bank_1'=4,'bank_2'=2,'zero'=4] {'bank_0'}, dimensions={0}, use_global_device_ids=true | all-gather | bytes 294912 | tf_op jit(solution)/shard_map/all_gather | solution.py:29
  63.6 0.1 copy.22
  63.7 12.7 %all-gather.2 = bf16[16,4,2048,2]{2,1,3,0:T(4,128)(2,1)S(1)} all-gather(bf16[8,4,2048,2]{2,1,3,0:T(4,128)(2,1)S(1)} %copy.22), channel_id=4, replica_groups=mesh['bank_0'=8,'bank_1'=4,'bank_2'=2,'zero'=4] {'bank_2'}, dimensions={0}, use_global_device_ids=true | all-gather | bytes 786432 | tf_op jit(solution)/shard_map/all_gather | solution.py:29
  76.5 0.3 copy.28
  76.7 0.5 copy.24
  77.3 0.2 reshape.20
  77.5 1.0 copy.25
  78.5 13.2 %all-gather.5.cloned.1.call-done = bf16[2,768,2048]{2,1,0:T(8,128)(2,1)} async-done(((bf16[2,768,512]{2,1,0:T(8,128)(2,1)}), bf16[2,768,2048]{2,1,0:T(8,128)(2,1)}) %all-gather.5.cloned.1.call-update) | async-done | bytes 6291472 | tf_op jit(solution)/shard_map/all_gather | solution.py:45
  91.7 6.6 %copy.30 = bf16[2,768,2048]{2,1,0:T(8,128)(2,1)} copy(bf16[2,768,2048]{2,1,0:T(8,128)(2,1)} %all-gather.5.cloned.1.call-done) | data formatting | bytes 12582912
  (4 shorter events, 0.0 us)
Async XLA Ops:
  7.2 84.5 %all-gather.5.cloned.1.call-start = ((), (), s32[]{:S(2)}) async-start(), calls=%async_computation.1 | async-start | bytes 7864320 | tf_op jit(solution)/shard_map/all_gather | solution.py:45
  10.6 10.4 %copy-start = (f32[2,768,512]{2,1,0:T(8,128)}, f32[2,768,512]{2,1,0:T(8,128)S(1)}, u32[]{:S(2)}) copy-start(f32[2,768,512]{2,1,0:T(8,128)S(1)} %get-tuple-element.33) | copy-start | bytes 9437188
  19.5 1.5 %copy-start.1 = (f32[2,768]{1,0:T(2,128)}, f32[2,768]{1,0:T(2,128)S(1)}, u32[]{:S(2)}) copy-start(f32[2,768]{1,0:T(2,128)S(1)} %broadcast_multiply_fusion) | copy-start | bytes 18436
  19.5 1.5 %copy-start.2 = (f32[512,2]{0,1:T(2,128)S(1)}, f32[512,2]{0,1:T(2,128)}, u32[]{:S(2)}) copy-start(f32[512,2]{0,1:T(2,128)} %param.6) | copy-start | bytes 12292
  19.5 1.5 %copy-start.3 = (f32[512]{0:T(512)S(1)}, f32[512]{0:T(512)}, u32[]{:S(2)}) copy-start(f32[512]{0:T(512)} %param.7) | copy-start | bytes 6148
Sparse Core Ops, SparseCore 0:
  21.1 70.5 all-gather.4
where the time goes:
time: 105 us
  blocking collectives  64.1 us (61%)
  between operations  14.1 us (13%)
  waiting for transfers between devices  13.2 us (13%)
  local copies, waits for them, and re-layouts  8.81 us (8%)
  other arithmetic  4.81 us (5%)
    all_gather x3, blocking collectives, all_blocks(): blocks = lax.all_gather(blocks, axes[k])  47.1 us
    all_gather x1, waiting for transfers between devices, shards(): ready_down = lax.all_gather(narrow_down, 'zero', axis=2, tiled=True)  13.2 us
    all_to_all x1, blocking collectives, copy_for_each(): lax.all_to_all(jnp.broadcast_to(x[None], (devices, *x.shape)), axis, 0, 0...  8.89 us
    all_gather x1, blocking collectives, shards(): row_router = lax.all_gather(part_router, 'zero', axis=0, tiled=True)  8.14 us
    unnamed x10, local copies, waits for them, and re-layouts  7.64 us
    reduce_sum x1, other arithmetic, shards(): total_down = of_everyone(jnp.sum(jnp.abs(latest_down), axis=2), 'zero')  3.34 us
  transfers between devices with their start and end apart: 1, of which 1 were waited for; matrix products, arithmetic and copies ran while one was open for 2% of the time, Pallas kernels for 0%

commit v1 on v0

v1 whole, which is shorter than its diff:
```python
import functools

import jax
import jax.numpy as jnp
from jax import lax
from jax.experimental import pallas as pl
from jax.experimental.pallas import tpu as pltpu
from jax.sharding import Mesh
from jax.sharding import PartitionSpec as P

D_MODEL = 2048
SIDES = 4
BANK = ("bank_0", "bank_1", "bank_2")


def shifted(x, by):
    return lax.ppermute(x, "zero", [(k, (k + by) % SIDES) for k in range(SIDES)])


def placed_into(shape, pieces, where, into=None):
    count = len(pieces)

    def kernel(*refs):
        src, out, sem = refs[:count], refs[-2], refs[-1]
        me = lax.axis_index("zero")
        copies = []
        for at, (expert, behind) in enumerate(where):
            width = src[at].shape[-1]
            col = pl.multiple_of(lax.rem(me - behind + SIDES, SIDES) * width, 512)
            copies.append(
                pltpu.make_async_copy(src[at], out.at[expert, :, pl.ds(col, width)], sem.at[at])
            )
        for copy in copies:
            copy.start()
        for copy in copies:
            copy.wait()

    args = list(pieces) + ([] if into is None else [into])
    specs = [pl.BlockSpec(memory_space=pl.ANY)] * count
    if into is not None:
        specs.append(pl.BlockSpec(memory_space=pltpu.HBM))
    size = sum(p.size * 2 for p in pieces)
    return pl.pallas_call(
        kernel,
        out_shape=jax.ShapeDtypeStruct(shape, jnp.bfloat16),
        in_specs=specs,
        out_specs=pl.BlockSpec(memory_space=pltpu.HBM),
        scratch_shapes=[pltpu.SemaphoreType.DMA((count,))],
        input_output_aliases={} if into is None else {count: 0},
        compiler_params=pltpu.CompilerParams(vmem_limit_bytes=1 << 20),
        cost_estimate=pl.CostEstimate(flops=size, bytes_accessed=2 * size, transcendentals=0),
        name="place",
    )(*args)


def shards(train_down, other_down, router_weight, router_gain):
    latest_down = 0.5 * other_down + 0.5 * train_down
    part = jnp.sum(jnp.abs(latest_down), axis=2)
    total = part + shifted(part, 1) + shifted(part, 2) + shifted(part, 3)
    scale_down = total / D_MODEL
    narrow = [
        (latest_down[e] / scale_down[e][:, None]).astype(jnp.bfloat16) for e in range(2)
    ]
    from_left = {0: shifted(narrow[0], 1)}
    from_right = {1: shifted(narrow[1], -1)}
    from_left[1] = shifted(narrow[1], 1)
    from_right[0] = shifted(narrow[0], -1)
    far0 = shifted(from_left[0], 1)
    far1 = shifted(from_right[1], -1)
    shape = (2, narrow[0].shape[0], D_MODEL)
    ready = placed_into(
        shape,
        [narrow[0], narrow[1], from_left[0], from_right[1], from_left[1], from_right[0]],
        [(0, 0), (1, 0), (0, 1), (1, -1), (1, 1), (0, -1)],
    )
    ready = placed_into(shape, [far0, far1], [(0, 2), (1, 2)], ready)

    part_router = (router_weight * router_gain[:, None]).astype(jnp.bfloat16)
    row_router = lax.all_gather(part_router.T, "zero", axis=1, tiled=True)
    every = lax.all_gather(row_router, ("bank_0", "bank_1", "bank_2"), axis=0, tiled=True)
    serve_router = every.T
    return (ready, scale_down, serve_router, latest_down)


def solution(mesh):
    split = Mesh(
        mesh.devices.reshape(8, 4, 2, mesh.shape["zero"]), ("bank_0", "bank_1", "bank_2", "zero")
    )
    placed = (P(BANK, None, "zero"), P(BANK, None, "zero"), P("zero", BANK), P("zero"))
    return jax.shard_map(
        shards,
        mesh=split,
        in_specs=placed,
        out_specs=(P(BANK, None, None), P(BANK, None), P(), P(BANK, None, "zero")),
        check_vma=False,
    )
```

time: 105 us -> 233 us (2.22)
  Pallas kernels: 0 us -> 97.6 us
  blocking collectives: 64.1 us -> 97.8 us
  starting transfers between devices: 0.04 us -> 13.8 us
  between operations: 14.1 us -> 0.73 us
  local copies, waits for them, and re-layouts: 8.81 us -> 4.12 us
    pallas_call x0 -> x2, Pallas kernels: none -> 97.6 us  [placed_into(): pl.pallas_call(kernel, out_shape=jax.ShapeDtypeStruct(shape, jnp.bfloat16...]
    all_gather x4 -> x2, blocking collectives: 55.3 us -> 97.8 us  [the longest x1 62.7 us: shards(): lax.all_gather(row_router, ('bank_0', 'bank_1', 'bank_2'), axis=0, tiled=...]
    ppermute x0 -> x9, waiting for transfers between devices: none -> 14.6 us  [shifted(): lax.ppermute(x, 'zero', [(k, (k + by) % SIDES) for k in range(SIDES)])]
    ppermute x0 -> x9, starting transfers between devices: none -> 13.8 us  [shifted(): lax.ppermute(x, 'zero', [(k, (k + by) % SIDES) for k in range(SIDES)])]
    all_gather x1 -> x0, waiting for transfers between devices: 13.2 us -> none  [shards(): ready_down = lax.all_gather(narrow_down, 'zero', axis=2, tiled=True)]
    all_to_all x1 -> x0, blocking collectives: 8.89 us -> none  [copy_for_each(): lax.all_to_all(jnp.broadcast_to(x[None], (devices, *x.shape)), axis, 0, 0...]
    unnamed x10, local copies, waits for them, and re-layouts: 7.64 us -> 4.1 us
  transfers between devices with their start and end apart: 1 -> 9, of which waited for: 1 -> 3; matrix products, arithmetic and copies ran while one was open for 2% -> 2% of each run, Pallas kernels for 0% -> 42%
where the time goes in v1:
time: 233 us; the launch traced here: 232 us
  blocking collectives  97.8 us (42%)
  Pallas kernels  97.6 us (42%)
  waiting for transfers between devices  14.6 us (6%)
  starting transfers between devices  13.8 us (6%)
  local copies, waits for them, and re-layouts  4.12 us (2%)
  other arithmetic  3.65 us (2%)
    pallas_call x2, Pallas kernels, placed_into(): pl.pallas_call(kernel, out_shape=jax.ShapeDtypeStruct(shape, jnp.bfloat16...  97.6 us
    all_gather x1, blocking collectives, shards(): lax.all_gather(row_router, ('bank_0', 'bank_1', 'bank_2'), axis=0, tiled=...  62.7 us
    all_gather x1, blocking collectives, shards(): row_router = lax.all_gather(part_router.T, 'zero', axis=1, tiled=True)  35.1 us
    ppermute x9, waiting for transfers between devices, shifted(): lax.ppermute(x, 'zero', [(k, (k + by) % SIDES) for k in range(SIDES)])  14.6 us
    ppermute x9, starting transfers between devices, shifted(): lax.ppermute(x, 'zero', [(k, (k + by) % SIDES) for k in range(SIDES)])  13.8 us
  transfers between devices with their start and end apart: 9, of which 3 were waited for; matrix products, arithmetic and copies ran while one was open for 2% of the time, Pallas kernels for 42%

profile of v1, /device:TPU:1, one launch (start us, length us, event | category | flops | bytes accessed | tf_op | source)
XLA Modules:
  0.0 232.4 jit_solution(12359393343071526170)
XLA Ops:
  0.6 3.3 %abs_reduce_fusion = (f32[2,768]{1,0:T(2,128)S(1)}, f32[2,768,512]{2,1,0:T(8,128)S(1)}) fusion(f32[2,768,512]{2,1,0:T(8,128)} %param.5, f32[2,768,512]{2,1,0:T(8,128)} %param.4), kind=kLoop, calls=%fused_computation | loop fusion | flops 3144192 | bytes 9443328 | tf_op jit(solution)/shard_map/reduce_sum | solution.py:58
  4.0 0.0 copy-start
  4.0 0.0 copy-start.2
  4.0 0.0 copy-start.3
  4.0 2.1 collective-permute-start
  6.1 2.5 %collective-permute-start.1 = (f32[2,768]{1,0:T(2,128)S(1)}, f32[2,768]{1,0:T(2,128)S(1)}, u32[]{:S(2)}, u32[]{:S(2)}) collective-permute-start(f32[2,768]{1,0:T(2,128)S(1)} %get-tuple-element.14), channel_id=1, source_target_pairs={{0,2},{1,3},{2,0},{3,1},{4,6},{5,7},{6,4},{7,5},{8,10},{9,11},{10,... | collective-permute-start | bytes 18440 | tf_op jit(solution)/shard_map/ppermute | solution.py:17
  8.6 1.2 collective-permute-start.2
  9.7 0.0 collective-permute-done
  9.7 0.4 collective-permute-done.1
  10.1 1.2 collective-permute-done.2
  11.4 0.0 copy-start.1
  11.4 0.3 fusion.1
  11.7 0.1 collective-permute-start.3
  11.8 2.7 %collective-permute-start.5 = (bf16[768,512]{1,0:T(8,128)(2,1)S(1)}, bf16[768,512]{1,0:T(8,128)(2,1)}, u32[]{:S(2)}, u32[]{:S(2)}) collective-permute-start(bf16[768,512]{1,0:T(8,128)(2,1)S(1)} %get-tuple-element.16.refs_1_), channel_id=1, source_target_pairs={{0,3},{1,0},{2,1},{3,2},{4,7},{5,4},{6,5},{7,6},{8,11},{9,8},{10,9... | collective-permute-start | bytes 2359304 | tf_op jit(solution)/shard_map/ppermute | solution.py:17
  14.4 0.0 collective-permute-start.7
  14.5 2.7 %collective-permute-start.8 = (bf16[768,512]{1,0:T(8,128)(2,1)S(1)}, bf16[768,512]{1,0:T(8,128)(2,1)}, u32[]{:S(2)}, u32[]{:S(2)}) collective-permute-start(bf16[768,512]{1,0:T(8,128)(2,1)S(1)} %get-tuple-element.17.refs_0_), channel_id=1, source_target_pairs={{0,3},{1,0},{2,1},{3,2},{4,7},{5,4},{6,5},{7,6},{8,11},{9,8},{10,9... | collective-permute-start | bytes 2359304 | tf_op jit(solution)/shard_map/ppermute | solution.py:17
  17.1 13.0 %collective-permute-done.3.refs_2_ = bf16[768,512]{1,0:T(8,128)(2,1)} collective-permute-done((bf16[768,512]{1,0:T(8,128)(2,1)S(1)}, bf16[768,512]{1,0:T(8,128)(2,1)}, u32[]{:S(2)}, u32[]{:S(2)}) %collective-permute-start.3) | collective-permute-done | bytes 786464 | tf_op jit(solution)/shard_map/ppermute | solution.py:17
  30.1 0.0 collective-permute-start.4
  30.1 0.0 collective-permute-done.5.refs_3_
  30.1 0.0 copy-done
  30.1 2.7 %collective-permute-start.6 = (bf16[768,512]{1,0:T(8,128)(2,1)}, bf16[768,512]{1,0:T(8,128)(2,1)S(1)}, u32[]{:S(2)}, u32[]{:S(2)}) collective-permute-start(bf16[768,512]{1,0:T(8,128)(2,1)} %collective-permute-done.5.refs_3_), channel_id=1, source_target_pairs={{0,3},{1,0},{2,1},{3,2},{4,7},{5,4},{6,5},{7,6},{8,11},{9,8},{10,9... | collective-permute-start | bytes 2359304 | tf_op jit(solution)/shard_map/ppermute | solution.py:17
  32.8 0.0 copy-done.2
  32.8 0.0 copy-done.3
  32.8 35.1 %all_gather.6 = bf16[2,2048]{1,0:T(2,128)(2,1)S(1)} all-gather(bf16[2,512]{1,0:T(2,128)(2,1)S(1)} %fusion.4), channel_id=1, replica_groups=mesh['bank_0'=8,'bank_1'=4,'bank_2'=2,'zero'=4] {'zero'}, dimensions={1}, use_global_device_ids=true | all-gather | bytes 10240 | tf_op jit(solution)/shard_map/all_gather | solution.py:79
  67.9 62.7 %all-gather = bf16[64,2,2048]{2,1,0:T(2,128)(2,1)} all-gather(bf16[1,2,2048]{2,1,0:T(2,128)(2,1)S(1)} %bitcast.17), channel_id=1, replica_groups=mesh['bank_0'=8,'bank_1'=4,'bank_2'=2,'zero'=4] {'bank_0','bank_1','bank..., dimensions={0}, use_global_device_ids=true | all-gather | bytes 532480 | tf_op jit(solution)/shard_map/all_gather | solution.py:80
  130.6 2.0 reshape.12
  132.7 0.0 copy-done.1
  132.7 2.0 copy.11
  134.7 0.0 collective-permute-done.7.refs_4_
  134.7 0.0 collective-permute-done.8.refs_5_
  134.7 96.4 %place.2.refs_2_ = bf16[2,768,2048]{2,1,0:T(8,128)(2,1)} custom-call(bf16[768,512]{1,0:T(8,128)(2,1)S(1)} %get-tuple-element.17.refs_0_, bf16[768,512]{1,0:T(8,128)(2,1)S(1)} %get-tuple-element.16.refs_1_, bf16[768,512]{1,0:T(8,128)(2,1)} %collective-permute-done.3.refs_2_, bf16[768,512]{1,0:T(8,128)(2,1)} %collective-permute-done.5.refs_3_, ...), custom_call_target="tpu_custom_call" | custom-call | flops 4718592 | bytes 9437184 | tf_op jit(solution)/shard_map/place/pallas_call | solution.py:43
  231.2 0.0 collective-permute-done.4.refs_0_
  231.2 0.0 collective-permute-done.6.refs_1_
  231.2 1.2 place.3
  (3 shorter events, 0.0 us)
Async XLA Ops:
  4.0 26.1 %copy-start = (f32[2,768,512]{2,1,0:T(8,128)}, f32[2,768,512]{2,1,0:T(8,128)S(1)}, u32[]{:S(2)}) copy-start(f32[2,768,512]{2,1,0:T(8,128)S(1)} %get-tuple-element.15) | copy-start | bytes 9437188
  4.0 28.8 %copy-start.2 = (f32[512,2]{0,1:T(2,128)S(1)}, f32[512,2]{0,1:T(2,128)}, u32[]{:S(2)}) copy-start(f32[512,2]{0,1:T(2,128)} %param.6) | copy-start | bytes 12292
  4.0 28.8 %copy-start.3 = (f32[512]{0:T(512)S(1)}, f32[512]{0:T(512)}, u32[]{:S(2)}) copy-start(f32[512]{0:T(512)} %param.7) | copy-start | bytes 6148
  4.0 5.7 %collective-permute-start = (f32[2,768]{1,0:T(2,128)S(1)}, f32[2,768]{1,0:T(2,128)S(1)}, u32[]{:S(2)}, u32[]{:S(2)}) collective-permute-start(f32[2,768]{1,0:T(2,128)S(1)} %get-tuple-element.14), channel_id=1, source_target_pairs={{0,1},{1,2},{2,3},{3,0},{4,5},{5,6},{6,7},{7,4},{8,9},{9,10},{10,1... | collective-permute-start | bytes 18440 | tf_op jit(solution)/shard_map/ppermute | solution.py:17
  6.1 4.0 %collective-permute-start.1 = (f32[2,768]{1,0:T(2,128)S(1)}, f32[2,768]{1,0:T(2,128)S(1)}, u32[]{:S(2)}, u32[]{:S(2)}) collective-permute-start(f32[2,768]{1,0:T(2,128)S(1)} %get-tuple-element.14), channel_id=1, source_target_pairs={{0,2},{1,3},{2,0},{3,1},{4,6},{5,7},{6,4},{7,5},{8,10},{9,11},{10,... | collective-permute-start | bytes 18440 | tf_op jit(solution)/shard_map/ppermute | solution.py:17
  8.6 2.8 %collective-permute-start.2 = (f32[2,768]{1,0:T(2,128)S(1)}, f32[2,768]{1,0:T(2,128)S(1)}, u32[]{:S(2)}, u32[]{:S(2)}) collective-permute-start(f32[2,768]{1,0:T(2,128)S(1)} %get-tuple-element.14), channel_id=1, source_target_pairs={{0,3},{1,0},{2,1},{3,2},{4,7},{5,4},{6,5},{7,6},{8,11},{9,8},{10,9... | collective-permute-start | bytes 18440 | tf_op jit(solution)/shard_map/ppermute | solution.py:17
  11.4 121.3 %copy-start.1 = (f32[2,768]{1,0:T(2,128)}, f32[2,768]{1,0:T(2,128)S(1)}, u32[]{:S(2)}) copy-start(f32[2,768]{1,0:T(2,128)S(1)} %add_multiply_fusion.1) | copy-start | bytes 18436
  11.7 18.4 %collective-permute-start.3 = (bf16[768,512]{1,0:T(8,128)(2,1)S(1)}, bf16[768,512]{1,0:T(8,128)(2,1)}, u32[]{:S(2)}, u32[]{:S(2)}) collective-permute-start(bf16[768,512]{1,0:T(8,128)(2,1)S(1)} %get-tuple-element.17.refs_0_), channel_id=1, source_target_pairs={{0,1},{1,2},{2,3},{3,0},{4,5},{5,6},{6,7},{7,4},{8,9},{9,10},{10,1... | collective-permute-start | bytes 2359304 | tf_op jit(solution)/shard_map/ppermute | solution.py:17
  11.8 18.3 %collective-permute-start.5 = (bf16[768,512]{1,0:T(8,128)(2,1)S(1)}, bf16[768,512]{1,0:T(8,128)(2,1)}, u32[]{:S(2)}, u32[]{:S(2)}) collective-permute-start(bf16[768,512]{1,0:T(8,128)(2,1)S(1)} %get-tuple-element.16.refs_1_), channel_id=1, source_target_pairs={{0,3},{1,0},{2,1},{3,2},{4,7},{5,4},{6,5},{7,6},{8,11},{9,8},{10,9... | collective-permute-start | bytes 2359304 | tf_op jit(solution)/shard_map/ppermute | solution.py:17
  14.4 120.3 %collective-permute-start.7 = (bf16[768,512]{1,0:T(8,128)(2,1)S(1)}, bf16[768,512]{1,0:T(8,128)(2,1)}, u32[]{:S(2)}, u32[]{:S(2)}) collective-permute-start(bf16[768,512]{1,0:T(8,128)(2,1)S(1)} %get-tuple-element.16.refs_1_), channel_id=1, source_target_pairs={{0,1},{1,2},{2,3},{3,0},{4,5},{5,6},{6,7},{7,4},{8,9},{9,10},{10,1... | collective-permute-start | bytes 2359304 | tf_op jit(solution)/shard_map/ppermute | solution.py:17
  14.5 120.3 %collective-permute-start.8 = (bf16[768,512]{1,0:T(8,128)(2,1)S(1)}, bf16[768,512]{1,0:T(8,128)(2,1)}, u32[]{:S(2)}, u32[]{:S(2)}) collective-permute-start(bf16[768,512]{1,0:T(8,128)(2,1)S(1)} %get-tuple-element.17.refs_0_), channel_id=1, source_target_pairs={{0,3},{1,0},{2,1},{3,2},{4,7},{5,4},{6,5},{7,6},{8,11},{9,8},{10,9... | collective-permute-start | bytes 2359304 | tf_op jit(solution)/shard_map/ppermute | solution.py:17
  30.1 201.1 %collective-permute-start.4 = (bf16[768,512]{1,0:T(8,128)(2,1)}, bf16[768,512]{1,0:T(8,128)(2,1)S(1)}, u32[]{:S(2)}, u32[]{:S(2)}) collective-permute-start(bf16[768,512]{1,0:T(8,128)(2,1)} %collective-permute-done.3.refs_2_), channel_id=1, source_target_pairs={{0,1},{1,2},{2,3},{3,0},{4,5},{5,6},{6,7},{7,4},{8,9},{9,10},{10,1... | collective-permute-start | bytes 2359304 | tf_op jit(solution)/shard_map/ppermute | solution.py:17
  30.1 201.1 %collective-permute-start.6 = (bf16[768,512]{1,0:T(8,128)(2,1)}, bf16[768,512]{1,0:T(8,128)(2,1)S(1)}, u32[]{:S(2)}, u32[]{:S(2)}) collective-permute-start(bf16[768,512]{1,0:T(8,128)(2,1)} %collective-permute-done.5.refs_3_), channel_id=1, source_target_pairs={{0,3},{1,0},{2,1},{3,2},{4,7},{5,4},{6,5},{7,6},{8,11},{9,8},{10,9... | collective-permute-start | bytes 2359304 | tf_op jit(solution)/shard_map/ppermute | solution.py:17

commit v2 on v1

v2 whole, which is shorter than its diff:
```python
import jax
import jax.numpy as jnp
from jax import lax
from jax.experimental import pallas as pl
from jax.experimental.pallas import tpu as pltpu
from jax.sharding import Mesh
from jax.sharding import PartitionSpec as P

D_MODEL = 2048
BANK = ("bank_0", "bank_1", "bank_2")


def shifted(x, axis, by):
    n = lax.axis_size(axis)
    return lax.ppermute(x, axis, [(k, (k + by) % n) for k in range(n)])


def in_turn(x, axis):
    n = lax.axis_size(axis)
    return [x] + [shifted(x, axis, -by) for by in range(1, n)]


def ordered(blocks, axis):
    n = lax.axis_size(axis)
    at = lax.axis_index(axis)
    full = jnp.zeros((n, *blocks[0].shape), blocks[0].dtype)
    for by, block in enumerate(blocks):
        full = lax.dynamic_update_index_in_dim(full, block, lax.rem(at + by, n), 0)
    return full


def placed_into(shape, pieces, where, into=None):
    count = len(pieces)

    def kernel(*refs):
        src, out = refs[:count], refs[-2 - count - 1]
        held, came, went = refs[-2 - count : -2], refs[-2], refs[-1]
        me, sides = lax.axis_index("zero"), lax.axis_size("zero")
        copies = []
        for at, (expert, behind) in enumerate(where):
            width = src[at].shape[-1]
            col = pl.multiple_of(lax.rem(me - behind + sides, sides) * width, width)
            copies.append(
                (
                    pltpu.make_async_copy(src[at], held[at], came.at[at]),
                    pltpu.make_async_copy(
                        held[at], out.at[expert, :, pl.ds(col, width)], went.at[at]
                    ),
                )
            )
        for come, _ in copies:
            come.start()
        for come, go in copies:
            come.wait()
            go.start()
        for _, go in copies:
            go.wait()

    args = list(pieces) + ([] if into is None else [into])
    specs = [pl.BlockSpec(memory_space=pl.ANY)] * count
    if into is not None:
        specs.append(pl.BlockSpec(memory_space=pltpu.HBM))
    size = sum(p.size * 2 for p in pieces)
    return pl.pallas_call(
        kernel,
        out_shape=jax.ShapeDtypeStruct(shape, jnp.bfloat16),
        in_specs=specs,
        out_specs=pl.BlockSpec(memory_space=pltpu.HBM),
        scratch_shapes=[pltpu.VMEM(p.shape, p.dtype) for p in pieces]
        + [pltpu.SemaphoreType.DMA((count,)), pltpu.SemaphoreType.DMA((count,))],
        input_output_aliases={} if into is None else {count: 0},
        compiler_params=pltpu.CompilerParams(vmem_limit_bytes=size + (1 << 20)),
        cost_estimate=pl.CostEstimate(flops=size, bytes_accessed=2 * size, transcendentals=0),
        name="place",
    )(*args)


def work(train_down, other_down, router_weight, router_gain):
    part_router = (router_weight * router_gain[:, None]).astype(jnp.bfloat16).T
    latest_down = 0.5 * other_down + 0.5 * train_down
    part = jnp.sum(jnp.abs(latest_down), axis=2)
    rows = part.shape[1]
    message = jnp.concatenate([part, part_router.astype(jnp.float32)], axis=1)
    messages = in_turn(message, "zero")
    total = sum(m[:, :rows] for m in messages)
    scale_down = total / D_MODEL
    narrow = [
        (latest_down[e] / scale_down[e][:, None]).astype(jnp.bfloat16) for e in range(2)
    ]
    left0 = shifted(narrow[0], "zero", 1)
    right1 = shifted(narrow[1], "zero", -1)
    left1 = shifted(narrow[1], "zero", 1)
    right0 = shifted(narrow[0], "zero", -1)
    far0 = shifted(left0, "zero", 1)
    far1 = shifted(right1, "zero", -1)
    shape = (2, rows, D_MODEL)
    ready = placed_into(
        shape,
        [narrow[0], narrow[1], left0, right1, left1, right0],
        [(0, 0), (1, 0), (0, 1), (1, -1), (1, 1), (0, -1)],
    )
    ready = placed_into(shape, [far0, far1], [(0, 2), (1, 2)], ready)

    row_router = ordered([m[:, rows:].astype(jnp.bfloat16) for m in messages], "zero")
    line = ordered(in_turn(row_router, "bank_0"), "bank_0")
    plane = ordered(in_turn(line, "bank_1"), "bank_1")
    every = ordered(in_turn(plane, "bank_2"), "bank_2")
    serve_router = every.transpose(3, 5, 2, 1, 0, 4).reshape(D_MODEL, -1)
    return (ready, scale_down, serve_router, latest_down)


def solution(mesh):
    split = Mesh(
        mesh.devices.reshape(8, 4, 2, mesh.shape["zero"]), ("bank_0", "bank_1", "bank_2", "zero")
    )
    placed = (P(BANK, None, "zero"), P(BANK, None, "zero"), P("zero", BANK), P("zero"))
    return jax.shard_map(
        work,
        mesh=split,
        in_specs=placed,
        out_specs=(P(BANK, None, None), P(BANK, None), P(), P(BANK, None, "zero")),
        check_vma=False,
    )
```

time: 233 us -> 74 us (0.32)
  the two profiles are of different devices: /device:TPU:1 before, /device:TPU:6 now
where the time goes in v2:
time: 74 us; the launch traced here: 73.9 us
  starting transfers between devices  34.3 us (46%)
  waiting for transfers between devices  21 us (28%)
  other arithmetic  7.14 us (10%)
  local copies, waits for them, and re-layouts  5.48 us (7%)
  Pallas kernels  4.82 us (7%)
  between operations  1.12 us (2%)
    ppermute x20, starting transfers between devices, shifted(): return lax.ppermute(x, axis, [(k, (k + by) % n) for k in range(n)])  34.3 us
    ppermute x20, waiting for transfers between devices, shifted(): return lax.ppermute(x, axis, [(k, (k + by) % n) for k in range(n)])  21 us
    reduce_sum x1, other arithmetic, work(): part = jnp.sum(jnp.abs(latest_down), axis=2)  4.94 us
    pallas_call x2, Pallas kernels, placed_into(): pl.pallas_call(kernel, out_shape=jax.ShapeDtypeStruct(shape, jnp.bfloat16...  4.82 us
    unnamed x8, local copies, waits for them, and re-layouts  2.95 us
    convert_element_type x1, other arithmetic, work(): (latest_down[e] / scale_down[e][:, None]).astype(jnp.bfloat16)  2.17 us
    dynamic_update_slice x17, local copies, waits for them, and re-layouts, ordered(): full = lax.dynamic_update_index_in_dim(full, block, lax.rem(at + by, n), 0)  2.13 us
  transfers between devices with their start and end apart: 20, of which 10 were waited for; matrix products, arithmetic and copies ran while one was open for 7% of the time, Pallas kernels for 5%

profile of v2, /device:TPU:6, one launch (start us, length us, event | category | flops | bytes accessed | tf_op | source)
XLA Modules:
  0.0 73.9 jit_solution(14731594931173718001)
XLA Ops:
  0.6 0.0 copy-start.1
  0.6 0.0 copy-start.2
  0.7 4.9 %abs_reduce_fusion = (f32[2,768]{1,0:T(2,128)S(1)}, f32[2,768,512]{2,1,0:T(8,128)}) fusion(f32[2,768,512]{2,1,0:T(8,128)} %param.5, f32[2,768,512]{2,1,0:T(8,128)} %param.4), kind=kLoop, calls=%fused_computation | loop fusion | flops 3144192 | bytes 9443328 | tf_op jit(solution)/shard_map/reduce_sum | solution.py:81
  5.6 0.0 copy-done.1
  5.6 0.0 copy-done.2
  5.6 2.3 %collective-permute-start.2 = (f32[2,1280]{1,0:T(2,128)S(1)}, f32[2,1280]{1,0:T(2,128)S(1)}, u32[]{:S(2)}, u32[]{:S(2)}) collective-permute-start(f32[2,1280]{1,0:T(2,128)S(1)} %pad_maximum_fusion), channel_id=1, source_target_pairs={{0,1},{1,2},{2,3},{3,0},{4,5},{5,6},{6,7},{7,4},{8,9},{9,10},{10,1... | collective-permute-start | bytes 30728 | tf_op jit(solution)/shard_map/ppermute | solution.py:15
  7.9 0.7 collective-permute-start.1
  8.6 0.2 collective-permute-start
  8.9 0.5 collective-permute-done.2
  9.4 3.7 %collective-permute-done.1 = f32[2,1280]{1,0:T(2,128)S(1)} collective-permute-done((f32[2,1280]{1,0:T(2,128)S(1)}, f32[2,1280]{1,0:T(2,128)S(1)}, u32[]{:S(2)}, u32[]{:S(2)}) %collective-permute-start.1) | collective-permute-done | bytes 10272 | tf_op jit(solution)/shard_map/ppermute | solution.py:15
  13.1 0.4 collective-permute-done
  13.5 0.0 copy-start
  13.5 2.2 %fusion.1 = (bf16[768,512]{1,0:T(8,128)(2,1)S(1)}, bf16[768,512]{1,0:T(8,128)(2,1)S(1)}) fusion(f32[2,768,512]{2,1,0:T(8,128)} %get-tuple-element.39, f32[768]{0:T(1024)S(1)} %get-tuple-element.36, f32[768]{0:T(1024)S(1)} %get-tuple-element.37), kind=kLoop, calls=%fused_computation.4 | loop fusion | flops 1572864 | bytes 4724736 | tf_op jit(solution)/shard_map/convert_element_type | solution.py:88
  15.7 0.7 collective-permute-start.3
  16.4 1.4 %collective-permute-start.5 = (bf16[768,512]{1,0:T(8,128)(2,1)S(1)}, bf16[768,512]{1,0:T(8,128)(2,1)}, u32[]{:S(2)}, u32[]{:S(2)}) collective-permute-start(bf16[768,512]{1,0:T(8,128)(2,1)S(1)} %get-tuple-element.40.refs_1_), channel_id=1, source_target_pairs={{0,3},{1,0},{2,1},{3,2},{4,7},{5,4},{6,5},{7,6},{8,11},{9,8},{10,9... | collective-permute-start | bytes 2359304 | tf_op jit(solution)/shard_map/ppermute | solution.py:15
  17.9 5.9 %collective-permute-start.9 = (bf16[4,2,512]{2,1,0:T(2,128)(2,1)S(1)}, bf16[4,2,512]{2,1,0:T(2,128)(2,1)S(1)}, u32[]{:S(2)}, u32[]{:S(2)}) collective-permute-start(bf16[4,2,512]{2,1,0:T(2,128)(2,1)S(1)} %constant_dynamic-update-slice_fusion), channel_id=1, source_target_pairs={{0,224},{32,0},{64,32},{96,64},{128,96},{160,128},{192,160},{224,1... | collective-permute-start | bytes 24584 | tf_op jit(solution)/shard_map/ppermute | solution.py:15
  23.8 1.5 %collective-permute-start.10 = (bf16[4,2,512]{2,1,0:T(2,128)(2,1)S(1)}, bf16[4,2,512]{2,1,0:T(2,128)(2,1)S(1)}, u32[]{:S(2)}, u32[]{:S(2)}) collective-permute-start(bf16[4,2,512]{2,1,0:T(2,128)(2,1)S(1)} %constant_dynamic-update-slice_fusion), channel_id=1, source_target_pairs={{0,192},{32,224},{64,0},{96,32},{128,64},{160,96},{192,128},{224,1... | collective-permute-start | bytes 24584 | tf_op jit(solution)/shard_map/ppermute | solution.py:15
  25.2 0.4 collective-permute-start.11
  25.7 0.0 collective-permute-done.9
  25.7 5.0 %collective-permute-start.12 = (bf16[4,2,512]{2,1,0:T(2,128)(2,1)S(1)}, bf16[4,2,512]{2,1,0:T(2,128)(2,1)S(1)}, u32[]{:S(2)}, u32[]{:S(2)}) collective-permute-start(bf16[4,2,512]{2,1,0:T(2,128)(2,1)S(1)} %constant_dynamic-update-slice_fusion), channel_id=1, source_target_pairs={{0,128},{32,160},{64,192},{96,224},{128,0},{160,32},{192,64},{224,... | collective-permute-start | bytes 24584 | tf_op jit(solution)/shard_map/ppermute | solution.py:15
  30.7 0.0 collective-permute-done.10
  30.7 1.2 %collective-permute-start.13 = (bf16[4,2,512]{2,1,0:T(2,128)(2,1)S(1)}, bf16[4,2,512]{2,1,0:T(2,128)(2,1)S(1)}, u32[]{:S(2)}, u32[]{:S(2)}) collective-permute-start(bf16[4,2,512]{2,1,0:T(2,128)(2,1)S(1)} %constant_dynamic-update-slice_fusion), channel_id=1, source_target_pairs={{0,96},{32,128},{64,160},{96,192},{128,224},{160,0},{192,32},{224,... | collective-permute-start | bytes 24584 | tf_op jit(solution)/shard_map/ppermute | solution.py:15
  31.9 0.0 collective-permute-done.11
  31.9 1.5 %collective-permute-start.14 = (bf16[4,2,512]{2,1,0:T(2,128)(2,1)S(1)}, bf16[4,2,512]{2,1,0:T(2,128)(2,1)S(1)}, u32[]{:S(2)}, u32[]{:S(2)}) collective-permute-start(bf16[4,2,512]{2,1,0:T(2,128)(2,1)S(1)} %constant_dynamic-update-slice_fusion), channel_id=1, source_target_pairs={{0,64},{32,96},{64,128},{96,160},{128,192},{160,224},{192,0},{224,... | collective-permute-start | bytes 24584 | tf_op jit(solution)/shard_map/ppermute | solution.py:15
  33.4 0.0 collective-permute-done.12
  33.4 1.7 %collective-permute-start.15 = (bf16[4,2,512]{2,1,0:T(2,128)(2,1)S(1)}, bf16[4,2,512]{2,1,0:T(2,128)(2,1)S(1)}, u32[]{:S(2)}, u32[]{:S(2)}) collective-permute-start(bf16[4,2,512]{2,1,0:T(2,128)(2,1)S(1)} %constant_dynamic-update-slice_fusion), channel_id=1, source_target_pairs={{0,32},{32,64},{64,96},{96,128},{128,160},{160,192},{192,224},{224... | collective-permute-start | bytes 24584 | tf_op jit(solution)/shard_map/ppermute | solution.py:15
  35.2 0.1 dynamic_update_slice.62
  35.3 2.1 %collective-permute-done.13 = bf16[4,2,512]{2,1,0:T(2,128)(2,1)S(1)} collective-permute-done((bf16[4,2,512]{2,1,0:T(2,128)(2,1)S(1)}, bf16[4,2,512]{2,1,0:T(2,128)(2,1)S(1)}, u32[]{:S(2)}, u32[]{:S(2)}) %collective-permute-start.13) | collective-permute-done | bytes 8224 | tf_op jit(solution)/shard_map/ppermute | solution.py:15
  37.4 1.8 %collective-permute-start.7 = (bf16[768,512]{1,0:T(8,128)(2,1)S(1)}, bf16[768,512]{1,0:T(8,128)(2,1)}, u32[]{:S(2)}, u32[]{:S(2)}) collective-permute-start(bf16[768,512]{1,0:T(8,128)(2,1)S(1)} %get-tuple-element.40.refs_1_), channel_id=1, source_target_pairs={{0,1},{1,2},{2,3},{3,0},{4,5},{5,6},{6,7},{7,4},{8,9},{9,10},{10,1... | collective-permute-start | bytes 2359304 | tf_op jit(solution)/shard_map/ppermute | solution.py:15
  39.2 0.0 collective-permute-done.14
  39.2 0.3 collective-permute-start.8
  39.5 0.0 collective-permute-done.15
  39.6 0.1 dynamic_update_slice.63
  39.7 0.1 dynamic_update_slice.64
  39.8 0.1 dynamic_update_slice.65
  39.9 0.1 dynamic_update_slice.66
  39.9 0.1 dynamic_update_slice.67
  40.0 0.1 dynamic_update_slice.68
  40.1 0.1 dynamic_update_slice.69
  40.2 3.3 %collective-permute-start.16 = (bf16[8,4,2,512]{3,0,2,1:T(8,128)(2,1)S(1)}, bf16[8,4,2,512]{3,0,2,1:T(8,128)(2,1)S(1)}, u32[]{:S(2)}, u32[]{:S(2)}) collective-permute-start(bf16[8,4,2,512]{3,0,2,1:T(8,128)(2,1)S(1)} %dynamic_update_slice.69), channel_id=1, source_target_pairs={{0,24},{8,0},{16,8},{24,16},{1,25},{9,1},{17,9},{25,17},{2,26},{10... | collective-permute-start | bytes 196616 | tf_op jit(solution)/shard_map/ppermute | solution.py:15
  43.5 1.9 %collective-permute-done.16 = bf16[8,4,2,512]{3,0,2,1:T(8,128)(2,1)S(1)} collective-permute-done((bf16[8,4,2,512]{3,0,2,1:T(8,128)(2,1)S(1)}, bf16[8,4,2,512]{3,0,2,1:T(8,128)(2,1)S(1)}, u32[]{:S(2)}, u32[]{:S(2)}) %collective-permute-start.16) | collective-permute-done | bytes 65568 | tf_op jit(solution)/shard_map/ppermute | solution.py:15
  45.4 2.5 %collective-permute-start.17 = (bf16[8,4,2,512]{3,0,2,1:T(8,128)(2,1)S(1)}, bf16[8,4,2,512]{3,0,2,1:T(8,128)(2,1)S(1)}, u32[]{:S(2)}, u32[]{:S(2)}) collective-permute-start(bf16[8,4,2,512]{3,0,2,1:T(8,128)(2,1)S(1)} %dynamic_update_slice.69), channel_id=1, source_target_pairs={{0,16},{8,24},{16,0},{24,8},{1,17},{9,25},{17,1},{25,9},{2,18},{10... | collective-permute-start | bytes 196616 | tf_op jit(solution)/shard_map/ppermute | solution.py:15
  47.9 3.4 %collective-permute-done.17 = bf16[8,4,2,512]{3,0,2,1:T(8,128)(2,1)S(1)} collective-permute-done((bf16[8,4,2,512]{3,0,2,1:T(8,128)(2,1)S(1)}, bf16[8,4,2,512]{3,0,2,1:T(8,128)(2,1)S(1)}, u32[]{:S(2)}, u32[]{:S(2)}) %collective-permute-start.17) | collective-permute-done | bytes 65568 | tf_op jit(solution)/shard_map/ppermute | solution.py:15
  51.4 0.7 collective-permute-start.18
  52.1 0.0 collective-permute-done.3.refs_2_
  52.1 3.0 %collective-permute-start.4 = (bf16[768,512]{1,0:T(8,128)(2,1)}, bf16[768,512]{1,0:T(8,128)(2,1)S(1)}, u32[]{:S(2)}, u32[]{:S(2)}) collective-permute-start(bf16[768,512]{1,0:T(8,128)(2,1)} %collective-permute-done.3.refs_2_), channel_id=1, source_target_pairs={{0,1},{1,2},{2,3},{3,0},{4,5},{5,6},{6,7},{7,4},{8,9},{9,10},{10,1... | collective-permute-start | bytes 2359304 | tf_op jit(solution)/shard_map/ppermute | solution.py:15
  55.1 0.0 collective-permute-done.5.refs_3_
  55.1 0.0 collective-permute-start.6
  55.1 1.9 %collective-permute-done.18 = bf16[8,4,2,512]{3,0,2,1:T(8,128)(2,1)S(1)} collective-permute-done((bf16[8,4,2,512]{3,0,2,1:T(8,128)(2,1)S(1)}, bf16[8,4,2,512]{3,0,2,1:T(8,128)(2,1)S(1)}, u32[]{:S(2)}, u32[]{:S(2)}) %collective-permute-start.18) | collective-permute-done | bytes 65568 | tf_op jit(solution)/shard_map/ppermute | solution.py:15
  57.0 0.0 copy-done
  57.0 0.1 collective-permute-start.19
  57.1 0.2 broadcast_in_dim.71
  57.4 0.2 copy_dynamic-update-slice_fusion.1
  57.6 1.2 %collective-permute-done.19 = bf16[4,8,4,2,512]{4,1,3,2,0:T(8,128)(2,1)} collective-permute-done((bf16[4,8,4,2,512]{4,1,3,2,0:T(8,128)(2,1)S(1)}, bf16[4,8,4,2,512]{4,1,3,2,0:T(8,128)(2,1)}, u32[]{:S(2)}, u32[]{:S(2)}) %collective-permute-start.19) | collective-permute-done | bytes 262176 | tf_op jit(solution)/shard_map/ppermute | solution.py:15
  58.8 1.2 %copy_dynamic-update-slice_fusion = bf16[2,4,8,4,2,512]{5,3,4,0,1,2:T(4,128)(2,1)S(1)} fusion(bf16[2,4,8,4,2,512]{5,3,4,0,1,2:T(4,128)(2,1)S(1)} %copy_dynamic-update-slice_fusion.1, s32[]{:T(128)S(6)} %select_n.75, bf16[1,4,8,4,2,512]{5,2,4,3,1,0:T(8,128)(2,1)} %bitcast.20), kind=kLoop, calls=%fused_computation.8 | loop fusion | bytes 524292 | tf_op jit(solution)/shard_map/jit(dynamic_update_index_in_dim)/dynamic_update_slice | solution.py:28
  59.9 0.9 %copy.105 = bf16[16,8,4,512]{3,1,2,0:T(8,128)(2,1)} copy(bf16[16,8,4,512]{3,2,1,0:T(4,128)(2,1)S(1)} %bitcast.53) | data formatting | bytes 1048576
  60.8 2.0 %copy.104 = bf16[2048,128]{1,0:T(8,128)(2,1)} copy(bf16[2048,128]{0,1:T(8,128)(2,1)} %bitcast.54) | data formatting | bytes 1048576
  62.9 0.0 collective-permute-done.7.refs_4_
  62.9 0.0 collective-permute-done.8.refs_5_
  62.9 3.5 %place.2.refs_2_ = bf16[2,768,2048]{2,1,0:T(8,128)(2,1)} custom-call(bf16[768,512]{1,0:T(8,128)(2,1)S(1)} %get-tuple-element.41.refs_0_, bf16[768,512]{1,0:T(8,128)(2,1)S(1)} %get-tuple-element.40.refs_1_, bf16[768,512]{1,0:T(8,128)(2,1)} %collective-permute-done.3.refs_2_, bf16[768,512]{1,0:T(8,128)(2,1)} %collective-permute-done.5.refs_3_, ...), custom_call_target="tpu_custom_call" | custom-call | flops 4718592 | bytes 9437184 | tf_op jit(solution)/shard_map/place/pallas_call | solution.py:64
  66.4 2.9 %collective-permute-done.4.refs_0_ = bf16[768,512]{1,0:T(8,128)(2,1)S(1)} collective-permute-done((bf16[768,512]{1,0:T(8,128)(2,1)}, bf16[768,512]{1,0:T(8,128)(2,1)S(1)}, u32[]{:S(2)}, u32[]{:S(2)}) %collective-permute-start.4) | collective-permute-done | bytes 786464 | tf_op jit(solution)/shard_map/ppermute | solution.py:15
  69.3 3.1 %collective-permute-done.6.refs_1_ = bf16[768,512]{1,0:T(8,128)(2,1)S(1)} collective-permute-done((bf16[768,512]{1,0:T(8,128)(2,1)}, bf16[768,512]{1,0:T(8,128)(2,1)S(1)}, u32[]{:S(2)}, u32[]{:S(2)}) %collective-permute-start.6) | collective-permute-done | bytes 786464 | tf_op jit(solution)/shard_map/ppermute | solution.py:15
  72.4 1.3 %place.3 = bf16[2,768,2048]{2,1,0:T(8,128)(2,1)} custom-call(bf16[768,512]{1,0:T(8,128)(2,1)S(1)} %collective-permute-done.4.refs_0_, bf16[768,512]{1,0:T(8,128)(2,1)S(1)} %collective-permute-done.6.refs_1_, bf16[2,768,2048]{2,1,0:T(8,128)(2,1)} %place.2.refs_2_), custom_call_target="tpu_custom_call", output_to_operand_aliasing={{}: (2, {})} | custom-call | flops 1572864 | bytes 3145728 | tf_op jit(solution)/shard_map/place/pallas_call | solution.py:64
  (23 shorter events, 0.3 us)
Async XLA Ops:
  0.6 5.0 %copy-start.1 = (f32[512,2]{0,1:T(2,128)S(1)}, f32[512,2]{0,1:T(2,128)}, u32[]{:S(2)}) copy-start(f32[512,2]{0,1:T(2,128)} %param.6) | copy-start | bytes 12292
  0.6 5.0 %copy-start.2 = (f32[512]{0:T(512)S(1)}, f32[512]{0:T(512)}, u32[]{:S(2)}) copy-start(f32[512]{0:T(512)} %param.7) | copy-start | bytes 6148
  5.6 3.8 %collective-permute-start.2 = (f32[2,1280]{1,0:T(2,128)S(1)}, f32[2,1280]{1,0:T(2,128)S(1)}, u32[]{:S(2)}, u32[]{:S(2)}) collective-permute-start(f32[2,1280]{1,0:T(2,128)S(1)} %pad_maximum_fusion), channel_id=1, source_target_pairs={{0,1},{1,2},{2,3},{3,0},{4,5},{5,6},{6,7},{7,4},{8,9},{9,10},{10,1... | collective-permute-start | bytes 30728 | tf_op jit(solution)/shard_map/ppermute | solution.py:15
  7.9 5.2 %collective-permute-start.1 = (f32[2,1280]{1,0:T(2,128)S(1)}, f32[2,1280]{1,0:T(2,128)S(1)}, u32[]{:S(2)}, u32[]{:S(2)}) collective-permute-start(f32[2,1280]{1,0:T(2,128)S(1)} %pad_maximum_fusion), channel_id=1, source_target_pairs={{0,2},{1,3},{2,0},{3,1},{4,6},{5,7},{6,4},{7,5},{8,10},{9,11},{10,... | collective-permute-start | bytes 30728 | tf_op jit(solution)/shard_map/ppermute | solution.py:15
  8.6 4.9 %collective-permute-start = (f32[2,1280]{1,0:T(2,128)S(1)}, f32[2,1280]{1,0:T(2,128)S(1)}, u32[]{:S(2)}, u32[]{:S(2)}) collective-permute-start(f32[2,1280]{1,0:T(2,128)S(1)} %pad_maximum_fusion), channel_id=1, source_target_pairs={{0,3},{1,0},{2,1},{3,2},{4,7},{5,4},{6,5},{7,6},{8,11},{9,8},{10,9... | collective-permute-start | bytes 30728 | tf_op jit(solution)/shard_map/ppermute | solution.py:15
  13.5 43.5 %copy-start = (f32[2,768]{1,0:T(2,128)}, f32[2,768]{1,0:T(2,128)S(1)}, u32[]{:S(2)}) copy-start(f32[2,768]{1,0:T(2,128)S(1)} %fusion.4) | copy-start | bytes 18436
  15.7 36.4 %collective-permute-start.3 = (bf16[768,512]{1,0:T(8,128)(2,1)S(1)}, bf16[768,512]{1,0:T(8,128)(2,1)}, u32[]{:S(2)}, u32[]{:S(2)}) collective-permute-start(bf16[768,512]{1,0:T(8,128)(2,1)S(1)} %get-tuple-element.41.refs_0_), channel_id=1, source_target_pairs={{0,1},{1,2},{2,3},{3,0},{4,5},{5,6},{6,7},{7,4},{8,9},{9,10},{10,1... | collective-permute-start | bytes 2359304 | tf_op jit(solution)/shard_map/ppermute | solution.py:15
  16.4 38.7 %collective-permute-start.5 = (bf16[768,512]{1,0:T(8,128)(2,1)S(1)}, bf16[768,512]{1,0:T(8,128)(2,1)}, u32[]{:S(2)}, u32[]{:S(2)}) collective-permute-start(bf16[768,512]{1,0:T(8,128)(2,1)S(1)} %get-tuple-element.40.refs_1_), channel_id=1, source_target_pairs={{0,3},{1,0},{2,1},{3,2},{4,7},{5,4},{6,5},{7,6},{8,11},{9,8},{10,9... | collective-permute-start | bytes 2359304 | tf_op jit(solution)/shard_map/ppermute | solution.py:15
  17.9 7.8 %collective-permute-start.9 = (bf16[4,2,512]{2,1,0:T(2,128)(2,1)S(1)}, bf16[4,2,512]{2,1,0:T(2,128)(2,1)S(1)}, u32[]{:S(2)}, u32[]{:S(2)}) collective-permute-start(bf16[4,2,512]{2,1,0:T(2,128)(2,1)S(1)} %constant_dynamic-update-slice_fusion), channel_id=1, source_target_pairs={{0,224},{32,0},{64,32},{96,64},{128,96},{160,128},{192,160},{224,1... | collective-permute-start | bytes 24584 | tf_op jit(solution)/shard_map/ppermute | solution.py:15
  23.8 7.0 %collective-permute-start.10 = (bf16[4,2,512]{2,1,0:T(2,128)(2,1)S(1)}, bf16[4,2,512]{2,1,0:T(2,128)(2,1)S(1)}, u32[]{:S(2)}, u32[]{:S(2)}) collective-permute-start(bf16[4,2,512]{2,1,0:T(2,128)(2,1)S(1)} %constant_dynamic-update-slice_fusion), channel_id=1, source_target_pairs={{0,192},{32,224},{64,0},{96,32},{128,64},{160,96},{192,128},{224,1... | collective-permute-start | bytes 24584 | tf_op jit(solution)/shard_map/ppermute | solution.py:15
  25.2 6.7 %collective-permute-start.11 = (bf16[4,2,512]{2,1,0:T(2,128)(2,1)S(1)}, bf16[4,2,512]{2,1,0:T(2,128)(2,1)S(1)}, u32[]{:S(2)}, u32[]{:S(2)}) collective-permute-start(bf16[4,2,512]{2,1,0:T(2,128)(2,1)S(1)} %constant_dynamic-update-slice_fusion), channel_id=1, source_target_pairs={{0,160},{32,192},{64,224},{96,0},{128,32},{160,64},{192,96},{224,1... | collective-permute-start | bytes 24584 | tf_op jit(solution)/shard_map/ppermute | solution.py:15
  25.7 7.7 %collective-permute-start.12 = (bf16[4,2,512]{2,1,0:T(2,128)(2,1)S(1)}, bf16[4,2,512]{2,1,0:T(2,128)(2,1)S(1)}, u32[]{:S(2)}, u32[]{:S(2)}) collective-permute-start(bf16[4,2,512]{2,1,0:T(2,128)(2,1)S(1)} %constant_dynamic-update-slice_fusion), channel_id=1, source_target_pairs={{0,128},{32,160},{64,192},{96,224},{128,0},{160,32},{192,64},{224,... | collective-permute-start | bytes 24584 | tf_op jit(solution)/shard_map/ppermute | solution.py:15
  30.7 6.7 %collective-permute-start.13 = (bf16[4,2,512]{2,1,0:T(2,128)(2,1)S(1)}, bf16[4,2,512]{2,1,0:T(2,128)(2,1)S(1)}, u32[]{:S(2)}, u32[]{:S(2)}) collective-permute-start(bf16[4,2,512]{2,1,0:T(2,128)(2,1)S(1)} %constant_dynamic-update-slice_fusion), channel_id=1, source_target_pairs={{0,96},{32,128},{64,160},{96,192},{128,224},{160,0},{192,32},{224,... | collective-permute-start | bytes 24584 | tf_op jit(solution)/shard_map/ppermute | solution.py:15
  31.9 7.3 %collective-permute-start.14 = (bf16[4,2,512]{2,1,0:T(2,128)(2,1)S(1)}, bf16[4,2,512]{2,1,0:T(2,128)(2,1)S(1)}, u32[]{:S(2)}, u32[]{:S(2)}) collective-permute-start(bf16[4,2,512]{2,1,0:T(2,128)(2,1)S(1)} %constant_dynamic-update-slice_fusion), channel_id=1, source_target_pairs={{0,64},{32,96},{64,128},{96,160},{128,192},{160,224},{192,0},{224,... | collective-permute-start | bytes 24584 | tf_op jit(solution)/shard_map/ppermute | solution.py:15
  33.4 6.2 %collective-permute-start.15 = (bf16[4,2,512]{2,1,0:T(2,128)(2,1)S(1)}, bf16[4,2,512]{2,1,0:T(2,128)(2,1)S(1)}, u32[]{:S(2)}, u32[]{:S(2)}) collective-permute-start(bf16[4,2,512]{2,1,0:T(2,128)(2,1)S(1)} %constant_dynamic-update-slice_fusion), channel_id=1, source_target_pairs={{0,32},{32,64},{64,96},{96,128},{128,160},{160,192},{192,224},{224... | collective-permute-start | bytes 24584 | tf_op jit(solution)/shard_map/ppermute | solution.py:15
  37.4 25.5 %collective-permute-start.7 = (bf16[768,512]{1,0:T(8,128)(2,1)S(1)}, bf16[768,512]{1,0:T(8,128)(2,1)}, u32[]{:S(2)}, u32[]{:S(2)}) collective-permute-start(bf16[768,512]{1,0:T(8,128)(2,1)S(1)} %get-tuple-element.40.refs_1_), channel_id=1, source_target_pairs={{0,1},{1,2},{2,3},{3,0},{4,5},{5,6},{6,7},{7,4},{8,9},{9,10},{10,1... | collective-permute-start | bytes 2359304 | tf_op jit(solution)/shard_map/ppermute | solution.py:15
  39.2 23.7 %collective-permute-start.8 = (bf16[768,512]{1,0:T(8,128)(2,1)S(1)}, bf16[768,512]{1,0:T(8,128)(2,1)}, u32[]{:S(2)}, u32[]{:S(2)}) collective-permute-start(bf16[768,512]{1,0:T(8,128)(2,1)S(1)} %get-tuple-element.41.refs_0_), channel_id=1, source_target_pairs={{0,3},{1,0},{2,1},{3,2},{4,7},{5,4},{6,5},{7,6},{8,11},{9,8},{10,9... | collective-permute-start | bytes 2359304 | tf_op jit(solution)/shard_map/ppermute | solution.py:15
  40.2 5.2 %collective-permute-start.16 = (bf16[8,4,2,512]{3,0,2,1:T(8,128)(2,1)S(1)}, bf16[8,4,2,512]{3,0,2,1:T(8,128)(2,1)S(1)}, u32[]{:S(2)}, u32[]{:S(2)}) collective-permute-start(bf16[8,4,2,512]{3,0,2,1:T(8,128)(2,1)S(1)} %dynamic_update_slice.69), channel_id=1, source_target_pairs={{0,24},{8,0},{16,8},{24,16},{1,25},{9,1},{17,9},{25,17},{2,26},{10... | collective-permute-start | bytes 196616 | tf_op jit(solution)/shard_map/ppermute | solution.py:15
  45.4 6.0 %collective-permute-start.17 = (bf16[8,4,2,512]{3,0,2,1:T(8,128)(2,1)S(1)}, bf16[8,4,2,512]{3,0,2,1:T(8,128)(2,1)S(1)}, u32[]{:S(2)}, u32[]{:S(2)}) collective-permute-start(bf16[8,4,2,512]{3,0,2,1:T(8,128)(2,1)S(1)} %dynamic_update_slice.69), channel_id=1, source_target_pairs={{0,16},{8,24},{16,0},{24,8},{1,17},{9,25},{17,1},{25,9},{2,18},{10... | collective-permute-start | bytes 196616 | tf_op jit(solution)/shard_map/ppermute | solution.py:15
  51.4 5.6 %collective-permute-start.18 = (bf16[8,4,2,512]{3,0,2,1:T(8,128)(2,1)S(1)}, bf16[8,4,2,512]{3,0,2,1:T(8,128)(2,1)S(1)}, u32[]{:S(2)}, u32[]{:S(2)}) collective-permute-start(bf16[8,4,2,512]{3,0,2,1:T(8,128)(2,1)S(1)} %dynamic_update_slice.69), channel_id=1, source_target_pairs={{0,8},{8,16},{16,24},{24,0},{1,9},{9,17},{17,25},{25,1},{2,10},{10... | collective-permute-start | bytes 196616 | tf_op jit(solution)/shard_map/ppermute | solution.py:15
  52.1 17.2 %collective-permute-start.4 = (bf16[768,512]{1,0:T(8,128)(2,1)}, bf16[768,512]{1,0:T(8,128)(2,1)S(1)}, u32[]{:S(2)}, u32[]{:S(2)}) collective-permute-start(bf16[768,512]{1,0:T(8,128)(2,1)} %collective-permute-done.3.refs_2_), channel_id=1, source_target_pairs={{0,1},{1,2},{2,3},{3,0},{4,5},{5,6},{6,7},{7,4},{8,9},{9,10},{10,1... | collective-permute-start | bytes 2359304 | tf_op jit(solution)/shard_map/ppermute | solution.py:15
  55.1 17.3 %collective-permute-start.6 = (bf16[768,512]{1,0:T(8,128)(2,1)}, bf16[768,512]{1,0:T(8,128)(2,1)S(1)}, u32[]{:S(2)}, u32[]{:S(2)}) collective-permute-start(bf16[768,512]{1,0:T(8,128)(2,1)} %collective-permute-done.5.refs_3_), channel_id=1, source_target_pairs={{0,3},{1,0},{2,1},{3,2},{4,7},{5,4},{6,5},{7,6},{8,11},{9,8},{10,9... | collective-permute-start | bytes 2359304 | tf_op jit(solution)/shard_map/ppermute | solution.py:15
  57.0 1.8 %collective-permute-start.19 = (bf16[4,8,4,2,512]{4,1,3,2,0:T(8,128)(2,1)S(1)}, bf16[4,8,4,2,512]{4,1,3,2,0:T(8,128)(2,1)}, u32[]{:S(2)}, u32[]{:S(2)}) collective-permute-start(bf16[4,8,4,2,512]{4,1,3,2,0:T(8,128)(2,1)S(1)} %bitcast_dynamic-update-slice_fusion), channel_id=1, source_target_pairs={{0,4},{4,0},{1,5},{5,1},{2,6},{6,2},{3,7},{7,3},{8,12},{12,8},{9,1... | collective-permute-start | bytes 786440 | tf_op jit(solution)/shard_map/ppermute | solution.py:15
